TPU v7x, 256 devices: a whole 4x4x8 slice. The times are simulated.
256 devices in a mesh: vocab: 256 (over x, y, z, core).
Axes of the slice: x: 4, y: 4, z: 8, core: 2. Of those that a mesh axis runs over, the one named last changes fastest.
Arguments:
- hidden: bfloat16 [2, 256, 3584], P(None, 'vocab'), may hold values from -256 to 256
- head_weight: bfloat16 [3584, 196608], P(None, 'vocab'), may hold values from -1 to 1
- teacher: bfloat16 [2, 256, 196608], P(None, None, 'vocab'), may hold values from 0 to 1
Outputs:
- token_loss: float32 [2, 256], P(None, 'vocab')
- hidden_grad: bfloat16 [2, 256, 3584], P(None, 'vocab')
- head_grad: bfloat16 [3584, 196608], P(None, 'vocab')
All inputs are finite; a program needn't handle non-finite values.
Results may differ from a plain program's by a relative error of at most 0.012.
Values may be sent and summed in bfloat16 or wider, within the bound.
A program may use at most 128 MiB of HBM per device.

v0:
```python
import jax
import jax.numpy as jnp
from jax import lax
from jax.sharding import Mesh
from jax.sharding import PartitionSpec as P

VOCAB = ("vocab_0", "vocab_1", "vocab_2", "vocab_3")


def gathered_once(value, axis):
    leaves = jax.tree.leaves(value)
    order = sorted(range(len(leaves)), key=lambda k: -leaves[k].size)
    width = (1, *leaves[order[0]].shape)[-1]
    lines = [
        jnp.pad(leaves[k].reshape(-1), (0, -leaves[k].size % width)).reshape(-1, width)
        for k in order
    ]
    both, at, found = (lax.all_gather(jnp.concatenate(lines), axis), 0, {})
    for k, line in zip(order, lines):
        slab = both[:, at : at + len(line)].reshape(len(both), -1)
        found[k] = slab[:, : leaves[k].size].reshape(-1, *leaves[k].shape)
        at += len(line)
    numbers = iter(range(len(leaves)))
    return jax.tree.map(lambda _: found[next(numbers)], value)


def joined_all(value, axes, combine):
    for axis in axes:
        pieces = gathered_once(value, axis)
        value = jax.tree.map(lambda part: part[0], pieces)
        for k in range(1, lax.axis_size(axis)):
            value = combine(value, jax.tree.map(lambda part: part[k], pieces))
    return value


def combine_rows(first, second):
    first_peak, first_total, first_mass, first_cross = first
    second_peak, second_total, second_mass, second_cross = second
    joined_peak = jnp.maximum(first_peak, second_peak)
    joined_total = first_total * jnp.exp(first_peak - joined_peak) + second_total * jnp.exp(
        second_peak - joined_peak
    )
    return (joined_peak, joined_total, first_mass + second_mass, first_cross + second_cross)


def finish(logit_block, target_block):
    target_wide = target_block.astype(jnp.float32)
    teacher_mass = jnp.sum(target_wide, axis=-1)
    cross_term = jnp.sum(target_wide * logit_block, axis=-1)
    peak_logit = jnp.max(logit_block, axis=-1)
    exp_total = jnp.sum(jnp.exp(logit_block - peak_logit[..., None]), axis=-1)
    peak_logit, exp_total, teacher_mass, cross_term = joined_all(
        (peak_logit, exp_total, teacher_mass, cross_term), VOCAB, combine_rows
    )
    log_norm = peak_logit + jnp.log(exp_total)
    token_loss = teacher_mass * log_norm - cross_term
    logit_grad = (
        teacher_mass[..., None] * jnp.exp(logit_block - log_norm[..., None]) - target_wide
    ).astype(jnp.bfloat16)
    return (token_loss, logit_grad)


def shards(hidden, head_weight, teacher):
    group_count, row_count, model_width = hidden.shape
    contract = (((1,), (1,)), ((), ()))
    shard_rows = lax.all_gather(hidden, VOCAB, axis=1, tiled=True)
    logits = jnp.einsum("crd,dv->crv", shard_rows, head_weight, preferred_element_type=jnp.float32)
    token_loss, logit_grad = finish(logits, teacher)
    row_total = lax.axis_size(VOCAB) * (group_count * row_count)
    per_group = row_total // group_count
    owner_count = per_group // row_count
    grad_block = logit_grad
    grad_block = (
        grad_block.reshape(group_count, owner_count, row_count, -1)
        .transpose(1, 0, 2, 3)
        .reshape(row_total, -1)
    )
    summed = lax.psum_scatter(
        lax.dot_general(grad_block, head_weight, contract, preferred_element_type=jnp.float32),
        VOCAB,
        scatter_dimension=0,
        tiled=True,
    )
    hidden_grad = summed.reshape(group_count, row_count, model_width).astype(jnp.bfloat16)
    weight_grad = jnp.zeros((model_width, head_weight.shape[1]), jnp.bfloat16)
    for group_index in range(group_count):
        product_term = lax.dot_general(
            shard_rows[group_index],
            logit_grad[group_index],
            (((0,), (0,)), ((), ())),
            preferred_element_type=jnp.float32,
        )
        weight_grad = (weight_grad.astype(jnp.float32) + product_term).astype(jnp.bfloat16)
    own_loss = lax.dynamic_slice_in_dim(token_loss, lax.axis_index(VOCAB) * row_count, row_count, 1)
    return (own_loss, hidden_grad, weight_grad)


def solution(mesh):
    split = Mesh(mesh.devices.reshape(4, 4, 8, 2), ("vocab_0", "vocab_1", "vocab_2", "vocab_3"))
    return jax.shard_map(
        shards,
        mesh=split,
        in_specs=(P(None, VOCAB, None), P(None, VOCAB), P(None, None, VOCAB)),
        out_specs=(P(None, VOCAB), P(None, VOCAB, None), P(None, VOCAB)),
        check_vma=False,
    )
```

profile of v0, /device:TPU:1, one launch (start us, length us, event | category | flops | bytes accessed | tf_op | source)
XLA Modules:
  0.0 362.0 jit_solution(12112623471678827758)
XLA Ops:
  7.2 0.0 all-gather.6.cloned.1.call-start
  7.2 0.7 all-gather.6.cloned.1.call-update
  7.9 0.0 copy-start
  7.9 123.5 %all-gather.6.cloned.1.call-done = bf16[2,256,3584]{2,0,1:T(2,128)(2,1)} async-done(((bf16[2,1,3584]{2,0,1:T(2,128)(2,1)}), bf16[2,256,3584]{2,0,1:T(2,128)(2,1)}) %all-gather.6.cloned.1.call-update) | async-done | bytes 3670032 | tf_op jit(solution)/shard_map/all_gather | solution.py:66
  131.4 6.8 %fusion.76 = (f32[2,256]{1,0:T(2,128)S(1)}, f32[2,256,768]{2,1,0:T(8,128)S(1)}) fusion(bf16[3584,768]{1,0:T(8,128)(2,1)} %param.4, bf16[2,256,3584]{2,0,1:T(2,128)(2,1)} %all-gather.6.cloned.1.call-done), kind=kOutput, calls=%fused_computation.155 | convolution fusion | flops 2818964992 | bytes 10749952 | tf_op jit(solution)/shard_map/crd,dv->crv/dot_general | solution.py:67
  138.2 0.0 copy-done
  138.2 0.7 exponential_reduce_fusion
  138.9 9.3 %all-gather = f32[32,256]{1,0:T(8,128)S(1)} all-gather(f32[8,256]{1,0:T(8,128)S(1)} %pad_maximum_fusion), channel_id=2, replica_groups=mesh['vocab_0'=4,'vocab_1'=4,'vocab_2'=8,'vocab_3'=2] {'vocab_0'}, dimensions={0}, use_global_device_ids=true | all-gather | bytes 40960 | tf_op jit(solution)/shard_map/all_gather | solution.py:18
  148.3 9.1 %all-gather.1 = f32[32,256]{1,0:T(8,128)S(1)} all-gather(f32[8,256]{1,0:T(8,128)S(1)} %pad_maximum_fusion.1), channel_id=3, replica_groups=mesh['vocab_0'=4,'vocab_1'=4,'vocab_2'=8,'vocab_3'=2] {'vocab_1'}, dimensions={0}, use_global_device_ids=true | all-gather | bytes 40960 | tf_op jit(solution)/shard_map/all_gather | solution.py:18
  157.4 18.4 %all-gather.2 = f32[64,256]{1,0:T(8,128)S(1)} all-gather(f32[8,256]{1,0:T(8,128)S(1)} %pad_maximum_fusion.2), channel_id=4, replica_groups=mesh['vocab_0'=4,'vocab_1'=4,'vocab_2'=8,'vocab_3'=2] {'vocab_2'}, dimensions={0}, use_global_device_ids=true | all-gather | bytes 73728 | tf_op jit(solution)/shard_map/all_gather | solution.py:18
  175.9 13.7 %all-gather.3 = f32[16,256]{1,0:T(8,128)S(1)} all-gather(f32[8,256]{1,0:T(8,128)S(1)} %pad_maximum_fusion.3), channel_id=5, replica_groups=mesh['vocab_0'=4,'vocab_1'=4,'vocab_2'=8,'vocab_3'=2] {'vocab_3'}, dimensions={0}, use_global_device_ids=true | all-gather | bytes 24576 | tf_op jit(solution)/shard_map/all_gather | solution.py:18
  189.7 0.4 fusion.4
  190.1 0.1 dynamic-slice_subtract_fusion
  190.2 0.6 copy.22
  190.8 0.8 copy.19
  191.6 0.3 reshape.111
  191.9 7.7 %fusion.77 = f32[512,3584]{1,0:T(8,128)} fusion(bf16[512,768]{1,0:T(8,128)(2,1)S(1)} %reshape.111, bf16[3584,768]{1,0:T(8,128)(2,1)} %param.4), kind=kOutput, calls=%fused_computation.156 | convolution fusion | flops 2818572288 | bytes 13631488 | tf_op jit(solution)/shard_map/dot_general | solution.py:79
  199.5 137.8 %all-reduce.2 = bf16[512,3584]{1,0:T(8,128)(2,1)} all-reduce(f32[512,3584]{1,0:T(8,128)} %fusion.77), channel_id=6, replica_groups=mesh['vocab_0'=4,'vocab_1'=4,'vocab_2'=8,'vocab_3'=2] {'vocab_0','vocab_..., use_global_device_ids=true, to_apply=%region_4.5.clone | all-reduce | flops 1835008 | bytes 11010048
  337.3 2.4 copy.18
  339.7 1.6 convolution_convert_fusion
  341.4 4.1 %fusion = bf16[3584,768]{0,1:T(8,128)(2,1)} fusion(bf16[768,3584]{1,0:T(8,128)(2,1)S(1)} %convolution_convert_fusion, bf16[2,256,3584]{2,1,0:T(8,128)(2,1)S(1)} %copy.18, bf16[2,256,768]{2,1,0:T(8,128)(2,1)S(1)} %fusion.4), kind=kOutput, calls=%fused_computation.2 | convolution fusion | flops 1417543680 | bytes 13238272 | tf_op jit(solution)/shard_map/dot_general | solution.py:87
  345.4 8.3 %copy.23 = bf16[3584,768]{1,0:T(8,128)(2,1)} copy(bf16[3584,768]{0,1:T(8,128)(2,1)} %fusion) | data formatting | bytes 11010048
  353.7 1.4 fusion.5
  (12 shorter events, 0.2 us)
Async XLA Ops:
  7.2 124.2 %all-gather.6.cloned.1.call-start = ((), (), s32[]{:S(2)}) async-start(), calls=%async_computation | async-start | bytes 3684352 | tf_op jit(solution)/shard_map/all_gather | solution.py:66
  7.9 130.2 %copy-start = (bf16[2,256,768]{2,1,0:T(8,128)(2,1)S(1)}, bf16[2,256,768]{2,1,0:T(8,128)(2,1)}, u32[]{:S(2)}) copy-start(bf16[2,256,768]{2,1,0:T(8,128)(2,1)} %param.5) | copy-start | bytes 2359300
Sparse Core Ops, SparseCore 0:
  11.8 119.5 all-gather.5
where the time goes:
time: 363 us; the launch traced here: 362 us
  blocking collectives  188 us (52%)
  waiting for transfers between devices  124 us (34%)
  matrix products  20.1 us (6%)
  between operations  14.1 us (4%)
  local copies, waits for them, and re-layouts  13.8 us (4%)
    unnamed x1, blocking collectives  138 us
    all_gather x1, waiting for transfers between devices, shards(): shard_rows = lax.all_gather(hidden, VOCAB, axis=1, tiled=True)  123 us
    all_gather x4, blocking collectives, gathered_once(): both, at, found = (lax.all_gather(jnp.concatenate(lines), axis), 0, {})  50.5 us
    unnamed x4, local copies, waits for them, and re-layouts  8.87 us
    dot_general x1, matrix products, shards(): lax.dot_general(grad_block, head_weight, contract, preferred_element_type...  7.67 us
  transfers between devices with their start and end apart: 1, of which 1 were waited for; matrix products, arithmetic and copies ran while one was open for 0% of the time, Pallas kernels for 0%

commit v1 on v0

v1 whole, which is shorter than its diff:
```python
import jax
import jax.numpy as jnp
from jax import lax
from jax.experimental import pallas as pl
from jax.experimental.pallas import tpu as pltpu
from jax.sharding import Mesh
from jax.sharding import PartitionSpec as P

AXES = ("x", "y", "z", "c")
NX, NY, NZ, NC = 4, 4, 8, 2
LINE = NZ * NC
PLANE = NX * NY
BF16, F32 = jnp.bfloat16, jnp.float32
MESH = pl.DeviceIdType.MESH
RING = (2, 1, 3, 0)
FAR_LINE = (8, 7, 9, 6, 10, 5, 11, 4, 12, 3, 13, 2, 14, 1, 15)


def main_kernel(
    hidden_ref, head_ref, teacher_ref, loss_ref, hgrad_ref, hid_out, grad_out,
    own, landed, spread, hid, head, teach, logit, grad, acc, half_out, half_in,
    ring_out, ring_in, side_out, side_in, line_out, line_in,
    stat_out, stat_line, stat_mid, stat_plane, stat_all,
    local_sem, p1_s, p1_r, d1_s, d1_r, d2_s, d2_r, pair_s, pair_r,
    sl_s, sl_r, sp_s, sp_r, sa_s, sa_r, hp_s, hp_r, rr_s, rr_r, rd_s, rd_r, zl_s, zl_r,
):
    me = {a: lax.axis_index(a) for a in AXES}
    core = me["c"]
    other = 1 - core
    sign = 1 - 2 * core
    rank = me["z"] * NC + core
    place = me["x"] * NY + me["y"]
    width = hidden_ref.shape[1]
    half = width // 2
    quarter = half // 2
    groups = hidden_ref.shape[0]
    started = []

    def send(src, dst, ssem, rsem, where):
        copy = pltpu.make_async_remote_copy(
            src_ref=src, dst_ref=dst, send_sem=ssem, recv_sem=rsem, device_id=where, device_id_type=MESH
        )
        copy.start()
        started.append(copy)
        return copy

    def line_peer(step):
        peer = lax.rem(rank + step, LINE)
        return peer, {"z": peer // NC, "c": lax.rem(peer, NC)}

    def plane_peer(step):
        peer = lax.rem(place + step, PLANE)
        return peer, {"x": peer // NY, "y": lax.rem(peer, NY)}

    def along(axis, step):
        return lax.rem(me[axis] + step + 4, 4)

    local = [
        pltpu.make_async_copy(head_ref, head, local_sem.at[0]),
        pltpu.make_async_copy(teacher_ref, teach, local_sem.at[1]),
    ]
    for copy in local:
        copy.start()

    barrier = pltpu.get_barrier_semaphore()
    for step in range(1, LINE):
        _, where = line_peer(step)
        pl.semaphore_signal(barrier, inc=1, device_id=where, device_id_type=MESH)
    for step in range(1, PLANE):
        _, where = plane_peer(step)
        pl.semaphore_signal(barrier, inc=1, device_id=where, device_id_type=MESH)

    mine = hidden_ref[...]
    for c in range(NC):
        own[c] = mine[:, c * half : (c + 1) * half]
    landed[rank] = own[core]
    pl.semaphore_wait(barrier, LINE - 1 + PLANE - 1)

    line = {}
    for step in FAR_LINE:
        peer, where = line_peer(step)
        line[step] = send(own.at[where["c"]], landed.at[rank], p1_s.at[step], p1_r.at[step], where)
    for step in FAR_LINE:
        line[step].wait_recv()
    for j in range(LINE):
        pair = landed[j].astype(F32)
        for g in range(groups):
            spread[g, j : j + 1] = pair[g : g + 1]
    for k in range(2):
        hid[2 * core + k, :, me["x"], me["y"]] = spread[:, :, k * quarter : (k + 1) * quarter].astype(BF16)

    first, second = ("x", "y"), ("y", "x")

    def block(k, i1, i2):
        i = (i1, i2) if k == 0 else (i2, i1)
        return hid.at[2 * core + k, :, i[0], i[1]]

    direct, ring, pair = {}, {}, {}
    for k in range(2):
        mine = block(k, me[first[k]], me[second[k]])
        for step in (2, 1, 3):
            direct[k, step] = send(
                mine, mine, d1_s.at[k, step], d1_r.at[k, step], {first[k]: along(first[k], step)}
            )
    for n, r in enumerate((0, 1, 3, 2)):
        for k in range(2):
            if r:
                direct[k, r].wait_recv()
            column = block(k, along(first[k], -r), me[second[k]])
            for d in range(2):
                ring[k, r, d] = send(
                    column, column, d2_s.at[k, r, d], d2_r.at[k, r, d], {second[k]: along(second[k], sign * (1 - 2 * d))}
                )
    for r in (0, 1, 3, 2):
        for k in range(2):
            ring[k, r, 0].wait_recv()
            column = block(k, along(first[k], -r), along(second[k], -sign))
            ring[k, r, 2] = send(
                column, column, d2_s.at[k, r, 2], d2_r.at[k, r, 2], {second[k]: along(second[k], sign)}
            )
    for r in (0, 1, 3, 2):
        for k in range(2):
            ring[k, r, 1].wait_recv()
            ring[k, r, 2].wait_recv()
            i1 = along(first[k], -r)
            column = hid.at[2 * core + k, :, i1] if k == 0 else hid.at[2 * core + k, :, :, i1]
            pair[k, r] = send(column, column, pair_s.at[k, r], pair_r.at[k, r], {"c": other})
    for copy in local:
        copy.wait()

    rows = groups * PLANE * LINE
    blocks = logit.shape[1] // 256

    def add_quarter(q, fresh):
        rows_q = hid[q].reshape(rows, quarter)
        for n in range(blocks):
            cols = slice(n * 256, (n + 1) * 256)
            term = jnp.dot(rows_q, head[q, :, cols], preferred_element_type=F32)
            logit[:, cols] = term if fresh else logit[:, cols] + term

    add_quarter(2 * core, True)
    add_quarter(2 * core + 1, False)
    for k in range(2):
        for r in (0, 1, 3, 2):
            pair[k, r].wait_recv()
        add_quarter(2 * other + k, False)
    keep_hid = pltpu.make_async_copy(hid, hid_out, local_sem.at[2])
    keep_hid.start()

    per = rows // groups
    lane = lax.broadcasted_iota(jnp.int32, (per, 128), 1)
    for g in range(groups):
        part = logit[g * per : (g + 1) * per]
        wide = teach[g].astype(F32)
        peak = jnp.max(part, axis=1, keepdims=True)
        total = jnp.sum(jnp.exp(part - peak), axis=1, keepdims=True)
        mass = jnp.sum(wide, axis=1, keepdims=True)
        cross = jnp.sum(wide * part, axis=1, keepdims=True)
        packed = jnp.where(lane == 0, peak, jnp.where(lane == 1, total, jnp.where(lane == 2, mass, cross)))
        stat_out[g] = packed.T[:4]
    stat_line[rank] = stat_out[core]
    line = {}
    for step in FAR_LINE:
        peer, where = line_peer(step)
        line[step] = send(stat_out.at[where["c"]], stat_line.at[rank], sl_s.at[step], sl_r.at[step], where)
    for step in FAR_LINE:
        line[step].wait_recv()

    def combined(ref, count):
        every = [ref[j] for j in range(count)]
        peak = every[0][0:1]
        for one in every[1:]:
            peak = jnp.maximum(peak, one[0:1])
        total = sum(one[1:2] * jnp.exp(one[0:1] - peak) for one in every)
        mass = sum(one[2:3] for one in every)
        cross = sum(one[3:4] for one in every)
        return peak, total, mass, cross

    stat_mid[...] = jnp.concatenate(combined(stat_line, LINE), axis=0)
    stat_plane[place] = stat_mid[...]
    plane = []
    for step in range(1, PLANE):
        _, where = plane_peer(step)
        plane.append(send(stat_mid, stat_plane.at[place], sp_s.at[step], sp_r.at[step], where))
    for copy in plane:
        copy.wait_recv()
    peak, total, mass, cross = combined(stat_plane, PLANE)
    norm = peak + jnp.log(total)
    stat_all[core] = jnp.concatenate([norm, mass, mass * norm - cross, peak], axis=0)
    swap = send(stat_all.at[core], stat_all.at[core], sa_s.at[0], sa_r.at[0], {"c": other})
    swap.wait_recv()

    token = lax.broadcasted_iota(jnp.int32, (1, per), 1)
    for g in range(groups):
        final = stat_all[g]
        loss = jnp.sum(jnp.where(token == place * LINE + rank, final[2:3], 0.0), axis=1, keepdims=True)
        loss_ref[g : g + 1] = loss
        tall = jnp.concatenate([final, jnp.zeros((124, per), F32)], axis=0).T
        part = logit[g * per : (g + 1) * per]
        grad[g] = (tall[:, 1:2] * jnp.exp(part - tall[:, 0:1]) - teach[g].astype(F32)).astype(BF16)
    keep_grad = pltpu.make_async_copy(grad, grad_out, local_sem.at[3])
    keep_grad.start()

    shape = (groups, NX, NY, LINE, quarter)

    def share(q):
        return lax.dot_general(
            grad[...].reshape(rows, -1), head[q], (((1,), (1,)), ((), ())), preferred_element_type=F32
        ).reshape(shape)

    over = []
    for k in range(2):
        half_out[k] = share(2 * other + k).astype(BF16)
        over.append(send(half_out.at[k], half_in.at[k], hp_s.at[k], hp_r.at[k], {"c": other}))
    for k in range(2):
        acc[k] = share(2 * core + k)

    def mine_at(k, i1, i2):
        i = (i1, i2) if k == 0 else (i2, i1)
        return acc[k, :, i[0], i[1]] + half_in[k, :, i[0], i[1]].astype(F32)

    ring, side = {}, {}

    def push(k, r, d, value, step):
        ring_out[k, r, d] = value.astype(BF16)
        ring[k, r, d] = send(
            ring_out.at[k, r, d], ring_in.at[k, r, d], rr_s.at[k, r, d], rr_r.at[k, r, d],
            {second[k]: along(second[k], step)},
        )

    for k in range(2):
        over[k].wait_recv()
        for r in RING:
            i1 = along(first[k], r)
            push(k, r, 0, mine_at(k, i1, along(second[k], 2)), sign)
            push(k, r, 1, mine_at(k, i1, along(second[k], -sign)), -sign)
    for r in RING:
        for k in range(2):
            i1 = along(first[k], r)
            ring[k, r, 0].wait_recv()
            push(k, r, 2, mine_at(k, i1, along(second[k], sign)) + ring_in[k, r, 0].astype(F32), sign)
    kept = {}
    for r in RING:
        for k in range(2):
            i1 = along(first[k], r)
            ring[k, r, 1].wait_recv()
            ring[k, r, 2].wait_recv()
            total = mine_at(k, i1, me[second[k]]) + ring_in[k, r, 1].astype(F32) + ring_in[k, r, 2].astype(F32)
            if r:
                side_out[k, r] = total.astype(BF16)
                side[k, r] = send(
                    side_out.at[k, r], side_in.at[k, r], rd_s.at[k, r], rd_r.at[k, r], {first[k]: i1}
                )
            else:
                kept[k] = total

    for k in range(2):
        for r in (2, 1, 3):
            side[k, r].wait_recv()
            kept[k] = kept[k] + side_in[k, r].astype(F32)
        spread[:, :, k * quarter : (k + 1) * quarter] = kept[k]
    for j in range(LINE):
        line_out[j] = jnp.concatenate([spread[g, j : j + 1] for g in range(groups)], axis=0).astype(BF16)
    line_in[core, me["z"]] = line_out[rank]
    line = {}
    for step in FAR_LINE:
        peer, where = line_peer(step)
        line[step] = send(line_out.at[peer], line_in.at[core, me["z"]], zl_s.at[step], zl_r.at[step], where)
    for step in FAR_LINE:
        line[step].wait_recv()
    for c in range(NC):
        total = line_in[c, 0].astype(F32)
        for z in range(1, NZ):
            total = total + line_in[c, z].astype(F32)
        hgrad_ref[:, c * half : (c + 1) * half] = total.astype(BF16)

    for copy in started:
        copy.wait_send()
    keep_hid.wait()
    keep_grad.wait()


def head_kernel(hid_ref, grad_ref, out_ref):
    rows = grad_ref.shape[0] * grad_ref.shape[1]
    states = hid_ref[0].reshape(rows, hid_ref.shape[-1])
    out_ref[...] = lax.dot_general(
        states, grad_ref[...].reshape(rows, -1), (((0,), (0,)), ((), ())), preferred_element_type=F32
    ).astype(BF16)


def shards(hidden, head_weight, teacher):
    groups, _, width = hidden.shape
    columns = head_weight.shape[1]
    tokens = teacher.shape[1]
    half, quarter = width // 2, width // 4
    plane = (groups, NX, NY, LINE, quarter)
    block = (groups, LINE, quarter)
    dma = pltpu.SemaphoreType.DMA
    vmem = pl.BlockSpec(memory_space=pltpu.VMEM)
    any_space = pl.BlockSpec(memory_space=pl.ANY)
    loss, hgrad, hid, grad = pl.pallas_call(
        main_kernel,
        name="gather_loss_reduce",
        out_shape=(
            jax.ShapeDtypeStruct((groups, 1), F32),
            jax.ShapeDtypeStruct((groups, width), BF16),
            jax.ShapeDtypeStruct((4, *plane), BF16),
            jax.ShapeDtypeStruct((groups, tokens, columns), BF16),
        ),
        in_specs=[vmem, any_space, any_space],
        out_specs=(vmem, vmem, any_space, any_space),
        scratch_shapes=[
            pltpu.VMEM((NC, groups, half), BF16),
            pltpu.VMEM((LINE, groups, half), BF16),
            pltpu.VMEM((groups, LINE, half), F32),
            pltpu.VMEM((4, *plane), BF16),
            pltpu.VMEM((4, quarter, columns), BF16),
            pltpu.VMEM((groups, tokens, columns), BF16),
            pltpu.VMEM((groups * tokens, columns), F32),
            pltpu.VMEM((groups, tokens, columns), BF16),
            pltpu.VMEM((2, *plane), F32),
            pltpu.VMEM((2, *plane), BF16),
            pltpu.VMEM((2, *plane), BF16),
            pltpu.VMEM((2, 4, 3, *block), BF16),
            pltpu.VMEM((2, 4, 3, *block), BF16),
            pltpu.VMEM((2, 4, *block), BF16),
            pltpu.VMEM((2, 4, *block), BF16),
            pltpu.VMEM((LINE, groups, half), BF16),
            pltpu.VMEM((NC, NZ, groups, half), BF16),
            pltpu.VMEM((groups, 4, tokens), F32),
            pltpu.VMEM((LINE, 4, tokens), F32),
            pltpu.VMEM((4, tokens), F32),
            pltpu.VMEM((PLANE, 4, tokens), F32),
            pltpu.VMEM((groups, 4, tokens), F32),
            dma((4,)),
            dma((LINE,)), dma((LINE,)),
            dma((2, 4)), dma((2, 4)),
            dma((2, 4, 3)), dma((2, 4, 3)),
            dma((2, 4)), dma((2, 4)),
            dma((LINE,)), dma((LINE,)),
            dma((PLANE,)), dma((PLANE,)),
            dma((1,)), dma((1,)),
            dma((2,)), dma((2,)),
            dma((2, 4, 3)), dma((2, 4, 3)),
            dma((2, 4)), dma((2, 4)),
            dma((LINE,)), dma((LINE,)),
        ],
        compiler_params=pltpu.CompilerParams(
            collective_id=0, has_side_effects=True, vmem_limit_bytes=56 * 1024 * 1024
        ),
    )(hidden.reshape(groups, width), head_weight.reshape(4, quarter, columns), teacher)
    head_grad = pl.pallas_call(
        head_kernel,
        name="head_gradient",
        grid=(4,),
        out_shape=jax.ShapeDtypeStruct((width, columns), BF16),
        in_specs=[
            pl.BlockSpec((1, *plane), lambda i: (i, 0, 0, 0, 0, 0)),
            pl.BlockSpec((groups, tokens, columns), lambda i: (0, 0, 0)),
        ],
        out_specs=pl.BlockSpec((quarter, columns), lambda i: (i, 0)),
    )(hid, grad)
    return (loss, hgrad.reshape(groups, 1, width), head_grad)


def solution(mesh):
    split = Mesh(mesh.devices.reshape(NX, NY, NZ, NC), AXES)
    return jax.shard_map(
        shards,
        mesh=split,
        in_specs=(P(None, AXES, None), P(None, AXES), P(None, None, AXES)),
        out_specs=(P(None, AXES), P(None, AXES, None), P(None, AXES)),
        check_vma=False,
    )
```

time: 363 us -> 82.9 us (0.23)
  blocking collectives: 188 us -> 0 us
  waiting for transfers between devices: 124 us -> 0 us
  Pallas kernels: 0 us -> 80.1 us
  matrix products: 20.1 us -> 0 us
  between operations: 14.1 us -> 0.65 us
  local copies, waits for them, and re-layouts: 13.8 us -> 1.83 us
    unnamed x1 -> x0, blocking collectives: 138 us -> none
    all_gather x1 -> x0, waiting for transfers between devices: 123 us -> none  [shards(): shard_rows = lax.all_gather(hidden, VOCAB, axis=1, tiled=True)]
    pallas_call x0 -> x2, Pallas kernels: none -> 80.1 us  [the longest x1 73.1 us: shards(): pl.pallas_call(main_kernel, name='gather_loss_reduce', out_shape=(jax.Sha...]
    all_gather x4 -> x0, blocking collectives: 50.5 us -> none  [gathered_once(): both, at, found = (lax.all_gather(jnp.concatenate(lines), axis), 0, {})]
    dot_general x4 -> x0, matrix products: 20.1 us -> none  [the longest x1 7.67 us: shards(): lax.dot_general(grad_block, head_weight, contract, preferred_element_type...]
    unnamed x4, local copies, waits for them, and re-layouts: 8.87 us -> 1.83 us
  transfers between devices with their start and end apart: 1 -> 0, of which waited for: 1 -> 0; matrix products, arithmetic and copies ran while one was open for 0% -> 0% of each run, Pallas kernels for 0% -> 0%
where the time goes in v1:
time: 82.9 us; the launch traced here: 82.6 us
  Pallas kernels  80.1 us (97%)
  local copies, waits for them, and re-layouts  1.83 us (2%)
    pallas_call x1, Pallas kernels, shards(): pl.pallas_call(main_kernel, name='gather_loss_reduce', out_shape=(jax.Sha...  73.1 us
    pallas_call x1, Pallas kernels, shards(): pl.pallas_call(head_kernel, name='head_gradient', grid=(4,), out_shape=ja...  7.05 us
    unnamed x4, local copies, waits for them, and re-layouts  1.83 us

profile of v1, /device:TPU:1, one launch (start us, length us, event | category | flops | bytes accessed | tf_op | source)
XLA Modules:
  0.0 82.6 jit_solution(2836744050585978904)
XLA Ops:
  0.6 73.1 %gather_loss_reduce.1 = (f32[2,1]{1,0:T(2,128)}, bf16[2,3584]{1,0:T(2,128)(2,1)}, bf16[4,2,4,4,16,896]{5,4,3,2,1,0:T(8,128)(2,1)}, bf16[2,256,768]{2,1,0:T(8,128)(2,1)}) custom-call(bf16[2,3584]{1,0:T(2,128)(2,1)} %bitcast.4, bf16[4,896,768]{2,1,0:T(8,128)(2,1)} %bitcast.3, bf16[2,256,768]{2,1,0:T(8,128)(2,1)} %teacher_ref.1), custom_call_target="tpu_custom_call" | custom-call | tf_op jit(solution)/shard_map/gather_loss_reduce/pallas_call | solution.py:301
  73.7 0.0 copy-start
  73.7 1.2 %copy.6 = f32[2,1]{0,1:T(1,128)} copy(f32[2,1]{1,0:T(2,128)} %get-tuple-element.11) | data formatting | bytes 16
  75.0 7.0 %head_gradient.1 = bf16[3584,768]{1,0:T(8,128)(2,1)} custom-call(bf16[4,2,4,4,16,896]{5,4,3,2,1,0:T(8,128)(2,1)} %get-tuple-element.9.hid_ref, bf16[2,256,768]{2,1,0:T(8,128)(2,1)} %get-tuple-element.10.grad_ref), custom_call_target="tpu_custom_call" | custom-call | tf_op jit(solution)/shard_map/head_gradient/pallas_call | solution.py:352
  82.0 0.0 copy-done
  82.0 0.6 copy.8
Async XLA Ops:
  73.7 8.3 %copy-start = (bf16[2,3584]{1,0:T(2,128)(2,1)S(1)}, bf16[2,3584]{1,0:T(2,128)(2,1)}, u32[]{:S(2)}) copy-start(bf16[2,3584]{1,0:T(2,128)(2,1)} %get-tuple-element.8) | copy-start | bytes 43012

commit v2 on v1

--- a/solution.py
+++ b/solution.py
@@ -17,7 +17,7 @@
 
 
 def main_kernel(
-    hidden_ref, head_ref, teacher_ref, loss_ref, hgrad_ref, hid_out, grad_out,
+    hidden_ref, head_ref, teacher_ref, loss_ref, hgrad_ref, head_grad_ref,
     own, landed, spread, hid, head, teach, logit, grad, acc, half_out, half_in,
     ring_out, ring_in, side_out, side_in, line_out, line_in,
     stat_out, stat_line, stat_mid, stat_plane, stat_all,
@@ -144,8 +144,6 @@
         for r in (0, 1, 3, 2):
             pair[k, r].wait_recv()
         add_quarter(2 * other + k, False)
-    keep_hid = pltpu.make_async_copy(hid, hid_out, local_sem.at[2])
-    keep_hid.start()
 
     per = rows // groups
     lane = lax.broadcasted_iota(jnp.int32, (per, 128), 1)
@@ -194,12 +192,10 @@
     for g in range(groups):
         final = stat_all[g]
         loss = jnp.sum(jnp.where(token == place * LINE + rank, final[2:3], 0.0), axis=1, keepdims=True)
-        loss_ref[g : g + 1] = loss
+        loss_ref[:, g : g + 1] = loss
         tall = jnp.concatenate([final, jnp.zeros((124, per), F32)], axis=0).T
         part = logit[g * per : (g + 1) * per]
         grad[g] = (tall[:, 1:2] * jnp.exp(part - tall[:, 0:1]) - teach[g].astype(F32)).astype(BF16)
-    keep_grad = pltpu.make_async_copy(grad, grad_out, local_sem.at[3])
-    keep_grad.start()
 
     shape = (groups, NX, NY, LINE, quarter)
 
@@ -220,6 +216,12 @@
         return acc[k, :, i[0], i[1]] + half_in[k, :, i[0], i[1]].astype(F32)
 
     ring, side = {}, {}
+
+    def head_gradient(q):
+        head_grad_ref[q * quarter : (q + 1) * quarter] = lax.dot_general(
+            hid[q].reshape(rows, quarter), grad[...].reshape(rows, -1), (((0,), (0,)), ((), ())),
+            preferred_element_type=F32,
+        ).astype(BF16)
 
     def push(k, r, d, value, step):
         ring_out[k, r, d] = value.astype(BF16)
@@ -234,11 +236,14 @@
             i1 = along(first[k], r)
             push(k, r, 0, mine_at(k, i1, along(second[k], 2)), sign)
             push(k, r, 1, mine_at(k, i1, along(second[k], -sign)), -sign)
+    head_gradient(0)
+    head_gradient(1)
     for r in RING:
         for k in range(2):
             i1 = along(first[k], r)
             ring[k, r, 0].wait_recv()
             push(k, r, 2, mine_at(k, i1, along(second[k], sign)) + ring_in[k, r, 0].astype(F32), sign)
+    head_gradient(2)
     kept = {}
     for r in RING:
         for k in range(2):
@@ -254,6 +259,7 @@
             else:
                 kept[k] = total
 
+    head_gradient(3)
     for k in range(2):
         for r in (2, 1, 3):
             side[k, r].wait_recv()
@@ -276,16 +282,6 @@
 
     for copy in started:
         copy.wait_send()
-    keep_hid.wait()
-    keep_grad.wait()
-
-
-def head_kernel(hid_ref, grad_ref, out_ref):
-    rows = grad_ref.shape[0] * grad_ref.shape[1]
-    states = hid_ref[0].reshape(rows, hid_ref.shape[-1])
-    out_ref[...] = lax.dot_general(
-        states, grad_ref[...].reshape(rows, -1), (((0,), (0,)), ((), ())), preferred_element_type=F32
-    ).astype(BF16)
 
 
 def shards(hidden, head_weight, teacher):
@@ -298,17 +294,16 @@
     dma = pltpu.SemaphoreType.DMA
     vmem = pl.BlockSpec(memory_space=pltpu.VMEM)
     any_space = pl.BlockSpec(memory_space=pl.ANY)
-    loss, hgrad, hid, grad = pl.pallas_call(
+    loss, hgrad, head_grad = pl.pallas_call(
         main_kernel,
         name="gather_loss_reduce",
         out_shape=(
-            jax.ShapeDtypeStruct((groups, 1), F32),
-            jax.ShapeDtypeStruct((groups, width), BF16),
-            jax.ShapeDtypeStruct((4, *plane), BF16),
-            jax.ShapeDtypeStruct((groups, tokens, columns), BF16),
+            pltpu.VMEM((1, groups), F32),
+            pltpu.VMEM((groups, width), BF16),
+            pltpu.VMEM((width, columns), BF16),
         ),
         in_specs=[vmem, any_space, any_space],
-        out_specs=(vmem, vmem, any_space, any_space),
+        out_specs=(vmem, vmem, vmem),
         scratch_shapes=[
             pltpu.VMEM((NC, groups, half), BF16),
             pltpu.VMEM((LINE, groups, half), BF16),
@@ -346,21 +341,10 @@
             dma((LINE,)), dma((LINE,)),
         ],
         compiler_params=pltpu.CompilerParams(
-            collective_id=0, has_side_effects=True, vmem_limit_bytes=56 * 1024 * 1024
+            collective_id=0, has_side_effects=True, vmem_limit_bytes=50 * 1024 * 1024
         ),
     )(hidden.reshape(groups, width), head_weight.reshape(4, quarter, columns), teacher)
-    head_grad = pl.pallas_call(
-        head_kernel,
-        name="head_gradient",
-        grid=(4,),
-        out_shape=jax.ShapeDtypeStruct((width, columns), BF16),
-        in_specs=[
-            pl.BlockSpec((1, *plane), lambda i: (i, 0, 0, 0, 0, 0)),
-            pl.BlockSpec((groups, tokens, columns), lambda i: (0, 0, 0)),
-        ],
-        out_specs=pl.BlockSpec((quarter, columns), lambda i: (i, 0)),
-    )(hid, grad)
-    return (loss, hgrad.reshape(groups, 1, width), head_grad)
+    return (loss.reshape(groups, 1), hgrad.reshape(groups, 1, width), head_grad)
 
 
 def solution(mesh):

time: 82.9 us -> 77.5 us (0.935)
  Pallas kernels: 80.1 us -> 73.1 us
  local copies, waits for them, and re-layouts: 1.83 us -> 3.56 us
    pallas_call x2 -> x1, Pallas kernels: 80.1 us -> 73.1 us  [shards(): pl.pallas_call(main_kernel, name='gather_loss_reduce', out_shape=(pltpu.V...]
    unnamed x4 -> x3, local copies, waits for them, and re-layouts: 1.83 us -> 3.56 us
where the time goes in v2:
time: 77.5 us; the launch traced here: 77.3 us
  Pallas kernels  73.1 us (94%)
  local copies, waits for them, and re-layouts  3.56 us (5%)
    pallas_call x1, Pallas kernels, shards(): pl.pallas_call(main_kernel, name='gather_loss_reduce', out_shape=(pltpu.V...  73.1 us
    unnamed x3, local copies, waits for them, and re-layouts  3.56 us

profile of v2, /device:TPU:1, one launch (start us, length us, event | category | flops | bytes accessed | tf_op | source)
XLA Modules:
  0.0 77.3 jit_solution(15650866293641510167)
XLA Ops:
  0.6 73.1 %gather_loss_reduce.1 = (f32[1,2]{1,0:T(1,128)S(1)}, bf16[2,3584]{1,0:T(2,128)(2,1)S(1)}, bf16[3584,768]{1,0:T(8,128)(2,1)S(1)}) custom-call(bf16[2,3584]{1,0:T(2,128)(2,1)} %bitcast.7, bf16[4,896,768]{2,1,0:T(8,128)(2,1)} %bitcast.6, bf16[2,256,768]{2,1,0:T(8,128)(2,1)} %teacher_ref.1), custom_call_target="tpu_custom_call" | custom-call | tf_op jit(solution)/shard_map/gather_loss_reduce/pallas_call | solution.py:297
  73.8 0.5 copy.9
  74.3 0.6 copy.10
  74.9 2.4 %copy.11 = bf16[3584,768]{1,0:T(8,128)(2,1)} copy(bf16[3584,768]{1,0:T(8,128)(2,1)S(1)} %get-tuple-element.11) | data formatting | bytes 11010048

commit v3 on v2

v3 whole, which is shorter than its diff:
```python
import jax
import jax.numpy as jnp
from jax import lax
from jax.experimental import pallas as pl
from jax.experimental.pallas import tpu as pltpu
from jax.sharding import Mesh
from jax.sharding import PartitionSpec as P

AXES = ("x", "y", "z", "c")
NX, NY, NZ, NC = 4, 4, 8, 2
LINE = NZ * NC
PLANE = NX * NY
BF16, F32 = jnp.bfloat16, jnp.float32
MESH = pl.DeviceIdType.MESH
RING = (2, 1, 3, 0)
FAR_PLANE = (10, 5, 7, 15, 13, 8, 2, 9, 11, 14, 6, 3, 1, 12, 4)
FAR_LINE = (8, 7, 9, 6, 10, 5, 11, 4, 12, 3, 13, 2, 14, 1, 15)


def main_kernel(
    hidden_ref, head_ref, teacher_ref, loss_ref, hgrad_ref, head_grad_ref,
    tokens, own, landed, spread, hid, head, teach, logit, grad, raised, raised_share, teach_share, column, half_out, half_in,
    ring_out, ring_in, side_out, side_in, line_out, line_in,
    stat_out, stat_line, stat_mid, stat_plane, stat_all,
    local_sem, sent, p1_r, d1_r, d2_r, pair_r, sl_r, sp_r, hp_r, rr_r, rd_r, zl_r,
):
    me = {a: lax.axis_index(a) for a in AXES}
    core = me["c"]
    other = 1 - core
    sign = 1 - 2 * core
    rank = me["z"] * NC + core
    place = me["x"] * NY + me["y"]
    width = hidden_ref.shape[1]
    half = width // 2
    quarter = half // 2
    groups, per, columns = teacher_ref.shape
    first, second = ("x", "y"), ("y", "x")

    def send(src, dst, ssem, rsem, where):
        copy = pltpu.make_async_remote_copy(
            src_ref=src, dst_ref=dst, send_sem=ssem, recv_sem=rsem, device_id=where, device_id_type=MESH
        )
        copy.start()
        return copy

    def wait_all(ref, sem):
        pltpu.make_async_copy(ref, ref, sem).wait()

    def line_peer(step):
        peer = lax.rem(rank + step, LINE)
        return peer, {"z": peer // NC, "c": lax.rem(peer, NC)}

    def plane_peer(step):
        peer = lax.rem(place + step, PLANE)
        return peer, {"x": peer // NY, "y": lax.rem(peer, NY)}

    def along(axis, step):
        return lax.rem(me[axis] + step + 4, 4)

    def product(ref, g, q):
        return lax.dot_general(
            ref[g], head[q], (((1,), (1,)), ((), ())), preferred_element_type=F32
        ).reshape(NX, NY, LINE, quarter)

    def share_teacher(g, q):
        teach_share[q, g] = product(teach, g, q)

    local = [
        pltpu.make_async_copy(hidden_ref, tokens, local_sem.at[0]),
        pltpu.make_async_copy(head_ref, head, local_sem.at[1]),
        pltpu.make_async_copy(teacher_ref, teach, local_sem.at[2]),
    ]
    for copy in local:
        copy.start()

    barrier = pltpu.get_barrier_semaphore()
    for step in FAR_LINE:
        _, where = line_peer(step)
        pl.semaphore_signal(barrier, inc=1, device_id=where, device_id_type=MESH)
    for step in FAR_PLANE:
        _, where = plane_peer(step)
        for c in (core, other):
            pl.semaphore_signal(barrier, inc=1, device_id={**where, "c": c}, device_id_type=MESH)

    local[0].wait()
    mine = tokens[...]
    for c in range(NC):
        own[c] = mine[:, c * half : (c + 1) * half]
    landed[rank] = own[core]
    pl.semaphore_wait(barrier, LINE - 1 + NC * (PLANE - 1))

    for step in FAR_LINE:
        peer, where = line_peer(step)
        send(own.at[where["c"]], landed.at[rank], sent.at[0], p1_r.at[0], where)
    for copy in local[1:]:
        copy.wait()
    share_teacher(0, 0)
    share_teacher(0, 1)
    share_teacher(0, 2)
    share_teacher(0, 3)
    share_teacher(1, 0)
    wait_all(landed.at[: LINE - 1], p1_r.at[0])
    for j in range(LINE):
        pair = landed[j].astype(F32)
        for g in range(groups):
            spread[g, j : j + 1] = pair[g : g + 1]
    for k in range(2):
        hid[2 * core + k, :, me["x"], me["y"]] = spread[:, :, k * quarter : (k + 1) * quarter].astype(BF16)

    direct, ring = {}, {}
    behind = (0, 1, 3, 2)

    def block(k, g, i1, i2):
        i = (i1, i2) if k == 0 else (i2, i1)
        return hid.at[2 * core + k, g, i[0], i[1]]

    def gather_first(g):
        for k in range(2):
            mine = block(k, g, me[first[k]], me[second[k]])
            for n in (1, 2, 3):
                direct[k, g, n] = send(
                    mine, mine, sent.at[1], d1_r.at[k, g, n], {first[k]: along(first[k], behind[n])}
                )

    def gather_ring(g, order, d):
        for n in order:
            for k in range(2):
                if n and d == 0:
                    direct[k, g, n].wait_recv()
                column = block(k, g, along(first[k], -behind[n]), me[second[k]])
                ring[k, g, n, d] = send(
                    column, column, sent.at[2], d2_r.at[k, g, n, d],
                    {second[k]: along(second[k], sign * (1 - 2 * d))},
                )

    def gather_relay(g):
        for n in range(4):
            for k in range(2):
                ring[k, g, n, 0].wait_recv()
                column = block(k, g, along(first[k], -behind[n]), along(second[k], -sign))
                send(column, column, sent.at[2], d2_r.at[k, g, n, 1], {second[k]: along(second[k], sign)})

    def gather_last(g):
        for n in range(4):
            for k in range(2):
                wait_all(ring_in.at[k, g, n, :2], d2_r.at[k, g, n, 1])
                i1 = along(first[k], -behind[n])
                column = hid.at[2 * core + k, g, i1] if k == 0 else hid.at[2 * core + k, g, :, i1]
                send(column, column, sent.at[3], pair_r.at[k, g], {"c": other})

    def states(q, g):
        return hid[q, g].reshape(per, quarter)

    def add_quarter(g, q, fresh):
        here = slice(g * per, (g + 1) * per)
        for n in range(columns // 256):
            cols = slice(n * 256, (n + 1) * 256)
            term = jnp.dot(states(q, g), head[q, :, cols], preferred_element_type=F32)
            logit[here, cols] = term if fresh else logit[here, cols] + term

    def logits_own(g):
        for k in range(2):
            add_quarter(g, 2 * core + k, k == 0)

    def logits_other():
        for k in range(2):
            for g in range(groups):
                wait_all(hid.at[0, g], pair_r.at[k, g])
            q = 2 * other + k
            every = hid[q].reshape(groups * per, quarter)
            for n in range(columns // 256):
                cols = slice(n * 256, (n + 1) * 256)
                logit[:, cols] += jnp.dot(every, head[q, :, cols], preferred_element_type=F32)

    def statistics():
        lane = lax.broadcasted_iota(jnp.int32, (per, 128), 1)
        for g in range(groups):
            part = logit[g * per : (g + 1) * per]
            wide = teach[g].astype(F32)
            peak = jnp.max(part, axis=1, keepdims=True)
            exponent = jnp.exp(part - peak)
            raised[g] = exponent.astype(BF16)
            total = jnp.sum(exponent, axis=1, keepdims=True)
            mass = jnp.sum(wide, axis=1, keepdims=True)
            cross = jnp.sum(wide * part, axis=1, keepdims=True)
            packed = jnp.where(lane == 0, peak, jnp.where(lane == 1, total, jnp.where(lane == 2, mass, cross)))
            column[g] = jnp.broadcast_to(peak, (per, 128))
            stat_out[g] = packed.T[:4]
        stat_line[rank] = stat_out[core]
        for step in FAR_LINE:
            peer, where = line_peer(step)
            send(stat_out.at[where["c"]], stat_line.at[rank], sent.at[4], sl_r.at[0], where)

    def combined(ref, slots):
        every = [ref[j] for j in slots]
        peak = every[0][0:1]
        for one in every[1:]:
            peak = jnp.maximum(peak, one[0:1])
        total = sum(one[1:2] * jnp.exp(one[0:1] - peak) for one in every)
        mass = sum(one[2:3] for one in every)
        cross = sum(one[3:4] for one in every)
        return peak, total, mass, cross

    def line_done():
        wait_all(stat_line.at[: LINE - 1], sl_r.at[0])
        stat_mid[...] = jnp.concatenate(combined(stat_line, range(LINE)), axis=0)
        slot = core * PLANE + place
        stat_plane[slot] = stat_mid[...]
        for step in (*FAR_PLANE, 0):
            _, where = plane_peer(step)
            for c in (core, other) if step else (other,):
                send(stat_mid, stat_plane.at[slot], sent.at[5], sp_r.at[0], {**where, "c": c})

    def plane_done():
        wait_all(stat_plane.at[: NC * PLANE - 1], sp_r.at[0])
        for g in range(groups):
            peak, total, mass, cross = combined(stat_plane, range(g * PLANE, (g + 1) * PLANE))
            norm = peak + jnp.log(total)
            stat_all[g] = jnp.concatenate([norm, mass, mass * norm - cross, peak], axis=0)

    def scales(g):
        final = stat_all[g]
        token = lax.broadcasted_iota(jnp.int32, (1, per), 1)
        loss = jnp.sum(jnp.where(token == place * LINE + rank, final[2:3], 0.0), axis=1, keepdims=True)
        loss_ref[:, g : g + 1] = loss
        tall = jnp.concatenate([final, jnp.zeros((124, per), F32)], axis=0).T
        peak = column[g, :, 0:1]
        lane = lax.broadcasted_iota(jnp.int32, (per, 128), 1)
        scale = tall[:, 1:2] * jnp.exp(peak - tall[:, 0:1])
        column[g] = jnp.where(lane == 0, tall[:, 0:1], jnp.where(lane == 1, tall[:, 1:2], scale))

    def gradient(g):
        tall = column[g]
        part = logit[g * per : (g + 1) * per]
        grad[g] = (tall[:, 1:2] * jnp.exp(part - tall[:, 0:1]) - teach[g].astype(F32)).astype(BF16)

    over = {}

    def share_raised(g, q):
        raised_share[q, g] = product(raised, g, q)

    def joined(g, q):
        scale = column[g, :, 2:3].reshape(NX, NY, LINE, 1)
        return raised_share[q, g] * scale - teach_share[q, g]

    def share_over(g, k):
        q = 2 * other + k
        half_out[k, g] = joined(g, q).astype(BF16)
        over[k, g] = send(half_out.at[k, g], half_in.at[k, g], sent.at[6], hp_r.at[k, g], {"c": other})

    def share_kept(g, k):
        q = 2 * core + k
        raised_share[q, g] = joined(g, q)

    hop = {}

    def mine_at(k, g, i1, i2):
        i = (i1, i2) if k == 0 else (i2, i1)
        return raised_share[2 * core + k, g, i[0], i[1]] + half_in[k, g, i[0], i[1]].astype(F32)

    def push(k, g, r, d, value, step):
        ring_out[k, g, r, d] = value.astype(BF16)
        hop[k, g, r, d] = send(
            ring_out.at[k, g, r, d], ring_in.at[k, g, r, d], sent.at[7], rr_r.at[k, g, r, min(d, 1)],
            {second[k]: along(second[k], step)},
        )

    def sum_start(g, k, d):
        if d == 0:
            over[k, g].wait_recv()
        for r in RING:
            i1 = along(first[k], r)
            push(k, g, r, d, mine_at(k, g, i1, along(second[k], -sign if d else 2)), -sign if d else sign)

    def sum_relay(g, k):
        for r in RING:
            i1 = along(first[k], r)
            hop[k, g, r, 0].wait_recv()
            carried = ring_in[k, g, r, 0].astype(F32)
            push(k, g, r, 2, mine_at(k, g, i1, along(second[k], sign)) + carried, sign)

    def sum_last(g, k):
        for r in RING:
            i1 = along(first[k], r)
            wait_all(ring_in.at[k, g, r, 1:], rr_r.at[k, g, r, 1])
            total = mine_at(k, g, i1, me[second[k]])
            total = total + ring_in[k, g, r, 1].astype(F32) + ring_in[k, g, r, 2].astype(F32)
            if r:
                side_out[k, g, r] = total.astype(BF16)
                send(side_out.at[k, g, r], side_in.at[k, g, r], sent.at[8], rd_r.at[k, g], {first[k]: i1})
            else:
                spread[g, :, k * quarter : (k + 1) * quarter] = total

    def sum_side(g):
        for k in range(2):
            here = slice(k * quarter, (k + 1) * quarter)
            total = spread[g, :, here]
            wait_all(side_in.at[k, g, 1:], rd_r.at[k, g])
            for r in RING[:3]:
                total = total + side_in[k, g, r].astype(F32)
            spread[g, :, here] = total

    def head_gradient(q):
        head_grad_ref[q * quarter : (q + 1) * quarter] = lax.dot_general(
            hid[q].reshape(groups * per, quarter), grad[...].reshape(groups * per, columns),
            (((0,), (0,)), ((), ())), preferred_element_type=F32,
        ).astype(BF16)

    gather_first(0)
    gather_ring(0, (0,), 0)
    gather_ring(0, (0,), 1)
    gather_first(1)
    share_teacher(1, 1)
    share_teacher(1, 2)
    gather_ring(0, (1, 2, 3), 0)
    gather_ring(0, (1, 2, 3), 1)
    gather_ring(1, (0, 1, 2, 3), 0)
    gather_ring(1, (0, 1, 2, 3), 1)
    share_teacher(1, 3)
    gather_relay(0)
    gather_relay(1)
    gather_last(0)
    logits_own(0)
    gather_last(1)
    logits_own(1)
    logits_other()
    statistics()
    share_raised(0, 2 * other)
    share_raised(0, 2 * core)
    share_raised(0, 2 * other + 1)
    share_raised(0, 2 * core + 1)
    line_done()
    share_raised(1, 2 * other)
    share_raised(1, 2 * core)
    share_raised(1, 2 * other + 1)
    share_raised(1, 2 * core + 1)
    plane_done()
    scales(0)
    share_over(0, 0)
    share_over(0, 1)
    scales(1)
    share_over(1, 0)
    share_over(1, 1)
    share_kept(0, 0)
    sum_start(0, 0, 0)
    share_kept(0, 1)
    sum_start(0, 1, 0)
    share_kept(1, 0)
    sum_start(1, 0, 0)
    share_kept(1, 1)
    sum_start(1, 1, 0)
    sum_start(0, 0, 1)
    sum_start(0, 1, 1)
    sum_relay(0, 0)
    sum_relay(0, 1)
    sum_start(1, 0, 1)
    sum_start(1, 1, 1)
    sum_relay(1, 0)
    sum_relay(1, 1)
    gradient(0)
    gradient(1)
    sum_last(0, 0)
    sum_last(0, 1)
    sum_last(1, 0)
    sum_last(1, 1)
    sum_side(0)
    sum_side(1)
    for j in range(LINE):
        line_out[j] = jnp.concatenate([spread[g, j : j + 1] for g in range(groups)], axis=0).astype(BF16)
    line_in[core, me["z"]] = line_out[rank]
    for step in FAR_LINE:
        peer, where = line_peer(step)
        send(line_out.at[peer], line_in.at[core, me["z"]], sent.at[9], zl_r.at[0], where)
    head_gradient(0)
    head_gradient(1)
    head_gradient(2)
    head_gradient(3)
    wait_all(line_out.at[: LINE - 1], zl_r.at[0])
    for c in range(NC):
        total = line_in[c, 0].astype(F32)
        for z in range(1, NZ):
            total = total + line_in[c, z].astype(F32)
        hgrad_ref[:, c * half : (c + 1) * half] = total.astype(BF16)

    for n, ref in enumerate(
        (
            landed.at[: LINE - 1], ring_in.at[:, :, 0], ring_in, hid.at[:2], stat_line.at[: LINE - 1],
            stat_plane.at[: NC * PLANE - 1], half_out, ring_out, side_out.at[:, :, 1:],
            line_out.at[: LINE - 1],
        )
    ):
        wait_all(ref, sent.at[n])


def place_kernel(loss_in, hgrad_in, head_in, loss_ref, hgrad_ref, head_ref, sem):
    copies = [
        pltpu.make_async_copy(head_in, head_ref, sem.at[0]),
        pltpu.make_async_copy(hgrad_in, hgrad_ref, sem.at[1]),
        pltpu.make_async_copy(loss_in, loss_ref, sem.at[2]),
    ]
    for copy in copies:
        copy.start()
    for copy in copies:
        copy.wait()


def shards(hidden, head_weight, teacher):
    groups, _, width = hidden.shape
    columns = head_weight.shape[1]
    count = teacher.shape[1]
    half, quarter = width // 2, width // 4
    plane = (groups, NX, NY, LINE, quarter)
    block = (LINE, quarter)
    dma = pltpu.SemaphoreType.DMA
    vmem = pl.BlockSpec(memory_space=pltpu.VMEM)
    any_space = pl.BlockSpec(memory_space=pl.ANY)
    results = pl.pallas_call(
        main_kernel,
        name="gather_loss_reduce",
        out_shape=(
            pltpu.VMEM((1, groups), F32),
            pltpu.VMEM((groups, width), BF16),
            pltpu.VMEM((width, columns), BF16),
        ),
        in_specs=[any_space, any_space, any_space],
        out_specs=(vmem, vmem, vmem),
        scratch_shapes=[
            pltpu.VMEM((groups, width), BF16),
            pltpu.VMEM((NC, groups, half), BF16),
            pltpu.VMEM((LINE, groups, half), BF16),
            pltpu.VMEM((groups, LINE, half), F32),
            pltpu.VMEM((4, *plane), BF16),
            pltpu.VMEM((4, quarter, columns), BF16),
            pltpu.VMEM((groups, count, columns), BF16),
            pltpu.VMEM((groups * count, columns), F32),
            pltpu.VMEM((groups, count, columns), BF16),
            pltpu.VMEM((groups, count, columns), BF16),
            pltpu.VMEM((4, *plane), F32),
            pltpu.VMEM((4, *plane), F32),
            pltpu.VMEM((groups, count, 128), F32),
            pltpu.VMEM((2, *plane), BF16),
            pltpu.VMEM((2, *plane), BF16),
            pltpu.VMEM((2, groups, 4, 3, *block), BF16),
            pltpu.VMEM((2, groups, 4, 3, *block), BF16),
            pltpu.VMEM((2, groups, 4, *block), BF16),
            pltpu.VMEM((2, groups, 4, *block), BF16),
            pltpu.VMEM((LINE, groups, half), BF16),
            pltpu.VMEM((NC, NZ, groups, half), BF16),
            pltpu.VMEM((groups, 4, count), F32),
            pltpu.VMEM((LINE, 4, count), F32),
            pltpu.VMEM((4, count), F32),
            pltpu.VMEM((NC * PLANE, 4, count), F32),
            pltpu.VMEM((groups, 4, count), F32),
            dma((3,)),
            dma((10,)),
            dma((1,)),
            dma((2, groups, 4)),
            dma((2, groups, 4, 2)),
            dma((2, groups)),
            dma((1,)),
            dma((1,)),
            dma((2, groups)),
            dma((2, groups, 4, 2)),
            dma((2, groups)),
            dma((1,)),
        ],
        compiler_params=pltpu.CompilerParams(
            collective_id=0, has_side_effects=True, vmem_limit_bytes=50 * 1024 * 1024
        ),
    )(hidden.reshape(groups, width), head_weight.reshape(4, quarter, columns), teacher)
    loss, hgrad, head_grad = pl.pallas_call(
        place_kernel,
        name="place_results",
        out_shape=(
            jax.ShapeDtypeStruct((1, groups), F32),
            jax.ShapeDtypeStruct((groups, width), BF16),
            jax.ShapeDtypeStruct((width, columns), BF16),
        ),
        in_specs=[vmem, vmem, vmem],
        out_specs=(any_space, any_space, any_space),
        scratch_shapes=[dma((3,))],
        compiler_params=pltpu.CompilerParams(vmem_limit_bytes=1024 * 1024),
    )(*(pltpu.with_memory_space_constraint(result, pltpu.VMEM) for result in results))
    return (loss.reshape(groups, 1), hgrad.reshape(groups, 1, width), head_grad)


def solution(mesh):
    split = Mesh(mesh.devices.reshape(NX, NY, NZ, NC), AXES)
    return jax.shard_map(
        shards,
        mesh=split,
        in_specs=(P(None, AXES, None), P(None, AXES), P(None, None, AXES)),
        out_specs=(P(None, AXES), P(None, AXES, None), P(None, AXES)),
        check_vma=False,
    )
```

time: 77.5 us -> 69.8 us (0.901)
  Pallas kernels: 73.1 us -> 68.9 us
  local copies, waits for them, and re-layouts: 3.56 us -> 0 us
    pallas_call x1, Pallas kernels: 73.1 us -> 66.4 us  [shards(): pl.pallas_call(main_kernel, name='gather_loss_reduce', out_shape=(pltpu.V...]
    unnamed x3 -> x0, local copies, waits for them, and re-layouts: 3.56 us -> none
    pallas_call x0 -> x1, Pallas kernels: none -> 2.48 us  [shards(): pl.pallas_call(place_kernel, name='place_results', out_shape=(jax.ShapeDt...]
where the time goes in v3:
time: 69.8 us; the launch traced here: 69.7 us
  Pallas kernels  68.9 us (99%)
  between operations  0.8 us (1%)
    pallas_call x1, Pallas kernels, shards(): pl.pallas_call(main_kernel, name='gather_loss_reduce', out_shape=(pltpu.V...  66.4 us
    pallas_call x1, Pallas kernels, shards(): pl.pallas_call(place_kernel, name='place_results', out_shape=(jax.ShapeDt...  2.48 us

profile of v3, /device:TPU:1, one launch (start us, length us, event | category | flops | bytes accessed | tf_op | source)
XLA Modules:
  0.0 69.7 jit_solution(16099638395230149019)
XLA Ops:
  0.6 66.4 %gather_loss_reduce.1 = (f32[1,2]{1,0:T(1,128)S(1)}, bf16[2,3584]{1,0:T(2,128)(2,1)S(1)}, bf16[3584,768]{1,0:T(8,128)(2,1)S(1)}) custom-call(bf16[2,3584]{1,0:T(2,128)(2,1)} %bitcast.5, bf16[4,896,768]{2,1,0:T(8,128)(2,1)} %bitcast.4, bf16[2,256,768]{2,1,0:T(8,128)(2,1)} %teacher_ref.1), custom_call_target="tpu_custom_call" | custom-call | tf_op jit(solution)/shard_map/gather_loss_reduce/pallas_call | solution.py:417
  67.0 2.5 %place_results.1 = (f32[1,2]{1,0:T(1,128)}, bf16[2,3584]{1,0:T(2,128)(2,1)}, bf16[3584,768]{1,0:T(8,128)(2,1)}) custom-call(f32[1,2]{1,0:T(1,128)S(1)} %get-tuple-element.9.loss_in, bf16[2,3584]{1,0:T(2,128)(2,1)S(1)} %get-tuple-element.10.hgrad_in, bf16[3584,768]{1,0:T(8,128)(2,1)S(1)} %get-tuple-element.11.head_in), custom_call_target="tpu_custom_call" | custom-call | tf_op jit(solution)/shard_map/place_results/pallas_call | solution.py:471

commit v4 on v3

--- a/solution.py
+++ b/solution.py
@@ -19,10 +19,10 @@
 
 def main_kernel(
     hidden_ref, head_ref, teacher_ref, loss_ref, hgrad_ref, head_grad_ref,
-    tokens, own, landed, spread, hid, head, teach, logit, grad, raised, raised_share, teach_share, column, half_out, half_in,
+    tokens, own, landed, spread, hid, head, teach, logit, grad, raised, raised_share, teach_share, weight, column, half_out, half_in,
     ring_out, ring_in, side_out, side_in, line_out, line_in,
     stat_out, stat_line, stat_mid, stat_plane, stat_all,
-    local_sem, sent, p1_r, d1_r, d2_r, pair_r, sl_r, sp_r, hp_r, rr_r, rd_r, zl_r,
+    local_sem, sent, p1_r, d1_r, d2_r, d2_l, pair_r, sl_r, sp_r, hp_r, rr_r, rd_r, zl_r,
 ):
     me = {a: lax.axis_index(a) for a in AXES}
     core = me["c"]
@@ -57,6 +57,10 @@
     def along(axis, step):
         return lax.rem(me[axis] + step + 4, 4)
 
+    def masses(g):
+        mass = jnp.sum(teach[g].astype(F32), axis=1, keepdims=True)
+        weight[g] = jnp.broadcast_to(mass, weight.shape[1:])
+
     def product(ref, g, q):
         return lax.dot_general(
             ref[g], head[q], (((1,), (1,)), ((), ())), preferred_element_type=F32
@@ -94,6 +98,8 @@
         send(own.at[where["c"]], landed.at[rank], sent.at[0], p1_r.at[0], where)
     for copy in local[1:]:
         copy.wait()
+    masses(0)
+    masses(1)
     share_teacher(0, 0)
     share_teacher(0, 1)
     share_teacher(0, 2)
@@ -119,7 +125,7 @@
             mine = block(k, g, me[first[k]], me[second[k]])
             for n in (1, 2, 3):
                 direct[k, g, n] = send(
-                    mine, mine, sent.at[1], d1_r.at[k, g, n], {first[k]: along(first[k], behind[n])}
+                    mine, mine, sent.at[1], d1_r.at[k, g, n - 1], {first[k]: along(first[k], behind[n])}
                 )
 
     def gather_ring(g, order, d):
@@ -129,7 +135,7 @@
                     direct[k, g, n].wait_recv()
                 column = block(k, g, along(first[k], -behind[n]), me[second[k]])
                 ring[k, g, n, d] = send(
-                    column, column, sent.at[2], d2_r.at[k, g, n, d],
+                    column, column, sent.at[2], d2_l.at[g, n] if d else d2_r.at[k, g, n],
                     {second[k]: along(second[k], sign * (1 - 2 * d))},
                 )
 
@@ -138,12 +144,12 @@
             for k in range(2):
                 ring[k, g, n, 0].wait_recv()
                 column = block(k, g, along(first[k], -behind[n]), along(second[k], -sign))
-                send(column, column, sent.at[2], d2_r.at[k, g, n, 1], {second[k]: along(second[k], sign)})
+                send(column, column, sent.at[2], d2_l.at[g, n], {second[k]: along(second[k], sign)})
 
     def gather_last(g):
         for n in range(4):
+            wait_all(ring_in.at[:, g, n, :2], d2_l.at[g, n])
             for k in range(2):
-                wait_all(ring_in.at[k, g, n, :2], d2_r.at[k, g, n, 1])
                 i1 = along(first[k], -behind[n])
                 column = hid.at[2 * core + k, g, i1] if k == 0 else hid.at[2 * core + k, g, :, i1]
                 send(column, column, sent.at[3], pair_r.at[k, g], {"c": other})
@@ -162,15 +168,10 @@
         for k in range(2):
             add_quarter(g, 2 * core + k, k == 0)
 
-    def logits_other():
+    def logits_other(g):
         for k in range(2):
-            for g in range(groups):
-                wait_all(hid.at[0, g], pair_r.at[k, g])
-            q = 2 * other + k
-            every = hid[q].reshape(groups * per, quarter)
-            for n in range(columns // 256):
-                cols = slice(n * 256, (n + 1) * 256)
-                logit[:, cols] += jnp.dot(every, head[q, :, cols], preferred_element_type=F32)
+            wait_all(hid.at[0, g], pair_r.at[k, g])
+            add_quarter(g, 2 * other + k, False)
 
     def statistics():
         lane = lax.broadcasted_iota(jnp.int32, (per, 128), 1)
@@ -178,10 +179,8 @@
             part = logit[g * per : (g + 1) * per]
             wide = teach[g].astype(F32)
             peak = jnp.max(part, axis=1, keepdims=True)
-            exponent = jnp.exp(part - peak)
-            raised[g] = exponent.astype(BF16)
-            total = jnp.sum(exponent, axis=1, keepdims=True)
-            mass = jnp.sum(wide, axis=1, keepdims=True)
+            total = jnp.sum(jnp.exp(part - peak), axis=1, keepdims=True)
+            mass = weight[g, :, 0:1]
             cross = jnp.sum(wide * part, axis=1, keepdims=True)
             packed = jnp.where(lane == 0, peak, jnp.where(lane == 1, total, jnp.where(lane == 2, mass, cross)))
             column[g] = jnp.broadcast_to(peak, (per, 128))
@@ -235,6 +234,10 @@
         grad[g] = (tall[:, 1:2] * jnp.exp(part - tall[:, 0:1]) - teach[g].astype(F32)).astype(BF16)
 
     over = {}
+
+    def raise_group(g):
+        part = logit[g * per : (g + 1) * per]
+        raised[g] = jnp.exp(part - column[g, :, 0:1]).astype(BF16)
 
     def share_raised(g, q):
         raised_share[q, g] = product(raised, g, q)
@@ -323,13 +326,16 @@
     logits_own(0)
     gather_last(1)
     logits_own(1)
-    logits_other()
+    logits_other(0)
+    logits_other(1)
     statistics()
+    raise_group(0)
     share_raised(0, 2 * other)
     share_raised(0, 2 * core)
     share_raised(0, 2 * other + 1)
     share_raised(0, 2 * core + 1)
     line_done()
+    raise_group(1)
     share_raised(1, 2 * other)
     share_raised(1, 2 * core)
     share_raised(1, 2 * other + 1)
@@ -438,6 +444,7 @@
             pltpu.VMEM((4, *plane), F32),
             pltpu.VMEM((4, *plane), F32),
             pltpu.VMEM((groups, count, 128), F32),
+            pltpu.VMEM((groups, count, 128), F32),
             pltpu.VMEM((2, *plane), BF16),
             pltpu.VMEM((2, *plane), BF16),
             pltpu.VMEM((2, groups, 4, 3, *block), BF16),
@@ -454,8 +461,9 @@
             dma((3,)),
             dma((10,)),
             dma((1,)),
+            dma((2, groups, 3)),
             dma((2, groups, 4)),
-            dma((2, groups, 4, 2)),
+            dma((groups, 4)),
             dma((2, groups)),
             dma((1,)),
             dma((1,)),

time: 69.8 us -> 70.1 us (level)
  no operation moved by 1% of the time
where the time goes in v4:
time: 70.1 us; the launch traced here: 70 us
  Pallas kernels  69.2 us (99%)
  between operations  0.8 us (1%)
    pallas_call x1, Pallas kernels, shards(): pl.pallas_call(main_kernel, name='gather_loss_reduce', out_shape=(pltpu.V...  66.7 us
    pallas_call x1, Pallas kernels, shards(): pl.pallas_call(place_kernel, name='place_results', out_shape=(jax.ShapeDt...  2.48 us

profile of v4, /device:TPU:1, one launch (start us, length us, event | category | flops | bytes accessed | tf_op | source)
XLA Modules:
  0.0 70.0 jit_solution(2800482478899757134)
XLA Ops:
  0.6 66.7 %gather_loss_reduce.1 = (f32[1,2]{1,0:T(1,128)S(1)}, bf16[2,3584]{1,0:T(2,128)(2,1)S(1)}, bf16[3584,768]{1,0:T(8,128)(2,1)S(1)}) custom-call(bf16[2,3584]{1,0:T(2,128)(2,1)} %bitcast.5, bf16[4,896,768]{2,1,0:T(8,128)(2,1)} %bitcast.4, bf16[2,256,768]{2,1,0:T(8,128)(2,1)} %teacher_ref.1), custom_call_target="tpu_custom_call" | custom-call | tf_op jit(solution)/shard_map/gather_loss_reduce/pallas_call | solution.py:423
  67.3 2.5 %place_results.1 = (f32[1,2]{1,0:T(1,128)}, bf16[2,3584]{1,0:T(2,128)(2,1)}, bf16[3584,768]{1,0:T(8,128)(2,1)}) custom-call(f32[1,2]{1,0:T(1,128)S(1)} %get-tuple-element.9.loss_in, bf16[2,3584]{1,0:T(2,128)(2,1)S(1)} %get-tuple-element.10.hgrad_in, bf16[3584,768]{1,0:T(8,128)(2,1)S(1)} %get-tuple-element.11.head_in), custom_call_target="tpu_custom_call" | custom-call | tf_op jit(solution)/shard_map/place_results/pallas_call | solution.py:479
